TPU v7x, 128 devices: a whole 4x4x4 slice. The times are simulated.
128 devices in a mesh: bank: 4 (over y_lo, core), zero: 32 (over z, y_hi, x).
Axes of the slice: x: 4, y: 4 (y_hi: 2, y_lo: 2; y = y_hi * 2 + y_lo), z: 4, core: 2. Of those that a mesh axis runs over, the one named last changes fastest.
Arguments:
- train_gate: float32 [128, 2048, 768], P('bank', 'zero'), may hold values from -0.25 to 0.25
- other_gate: bfloat16 [128, 2048, 768], P('bank', 'zero'), may hold values from -0.0625 to 0.0625
- train_up: float32 [128, 2048, 768], P('bank', 'zero'), may hold values from -0.25 to 0.25
- other_up: bfloat16 [128, 2048, 768], P('bank', 'zero'), may hold values from -0.0625 to 0.0625
- router_weight: float32 [2048, 128], P('zero', 'bank'), may hold values from -0.125 to 0.125
- router_gain: float32 [2048], P('zero'), may hold values from 0.25 to 1.75
Outputs:
- ready_gate: bfloat16 [128, 2048, 768], P(('bank', 'zero'))
- ready_up: bfloat16 [128, 2048, 768], P(('bank', 'zero'))
- scale_gate: float32 [128, 768], P(('bank', 'zero'))
- scale_up: float32 [128, 768], P(('bank', 'zero'))
- serve_router: bfloat16 [2048, 128], replicated
All inputs are finite; a program needn't handle non-finite values.
Results may differ from a plain program's by a relative error of at most 0.0075.
Values may be sent and summed in bfloat16 or wider, within the bound.
No kernel may reach another device: no remote copies, remote signals or barrier semaphores. Data moves between devices by JAX's collectives and lax.ppermute only.
A program may use at most 128 MiB of HBM per device.

v0:
```python
import jax
import jax.numpy as jnp
from jax import lax
from jax.sharding import PartitionSpec as P


def regrouped(train, other):
    latest = (train + other.astype(jnp.float32)).astype(jnp.bfloat16)
    return lax.all_to_all(latest, "zero", split_axis=0, concat_axis=1, tiled=True)


def normalised(pieces):
    wide = pieces.astype(jnp.float32)
    scale = jnp.sqrt(jnp.sum(wide * wide, axis=1))
    return ((wide / scale[:, None, :]).astype(jnp.bfloat16), scale)


def body(train_gate, other_gate, train_up, other_up, router_weight, router_gain):
    gate = regrouped(train_gate, other_gate)
    up = regrouped(train_up, other_up)
    part_router = (router_weight * router_gain[:, None]).astype(jnp.bfloat16)
    serve_router = lax.all_gather(part_router, "zero", axis=0, tiled=True)
    serve_router = lax.all_gather(serve_router, "bank", axis=1, tiled=True)
    ready_gate, scale_gate = normalised(gate)
    ready_up, scale_up = normalised(up)
    return (ready_gate, ready_up, scale_gate, scale_up, serve_router)


def solution(mesh):
    placed = (
        P("bank", "zero", None),
        P("bank", "zero", None),
        P("bank", "zero", None),
        P("bank", "zero", None),
        P("zero", "bank"),
        P("zero"),
    )
    return jax.shard_map(
        body,
        mesh=mesh,
        in_specs=placed,
        out_specs=(
            P(("bank", "zero"), None, None),
            P(("bank", "zero"), None, None),
            P(("bank", "zero"), None),
            P(("bank", "zero"), None),
            P(),
        ),
        check_vma=False,
    )
```

profile of v0, /device:TPU:1, one launch (start us, length us, event | category | flops | bytes accessed | tf_op | source)
XLA Modules:
  0.0 215.3 jit_solution(7930058115264093325)
XLA Ops:
  0.6 6.4 %add_convert_fusion = bf16[32,64,768]{2,1,0:T(8,128)(2,1)} fusion(f32[32,64,768]{2,1,0:T(8,128)} %param.8, bf16[32,64,768]{2,1,0:T(8,128)(2,1)} %param.9), kind=kLoop, calls=%fused_computation.5 | loop fusion | flops 4718592 | bytes 12582912 | tf_op jit(solution)/shard_map/convert_element_type | solution.py:8
  7.0 11.3 %all-to-all-start.1 = ((bf16[32,64,768]{2,1,0:T(8,128)(2,1)}), bf16[32,64,768]{2,1,0:T(8,128)(2,1)S(1)}, u32[]{:S(2)}, u32[]{:S(2)}) async-start(bf16[32,64,768]{2,1,0:T(8,128)(2,1)} %add_convert_fusion), calls=%async_computation.1 | async-start | bytes 6291456 | tf_op jit(solution)/shard_map/all_to_all | solution.py:9
  18.4 6.4 %add_convert_fusion.1 = bf16[32,64,768]{2,1,0:T(8,128)(2,1)} fusion(f32[32,64,768]{2,1,0:T(8,128)} %param.6, bf16[32,64,768]{2,1,0:T(8,128)(2,1)} %param.7), kind=kLoop, calls=%fused_computation.7 | loop fusion | flops 4718592 | bytes 12582912 | tf_op jit(solution)/shard_map/convert_element_type | solution.py:8
  24.8 0.0 copy-start.1
  24.8 0.0 copy-start.2
  24.8 34.0 %all-to-all-done.1 = bf16[32,64,768]{2,1,0:T(8,128)(2,1)S(1)} async-done(((bf16[32,64,768]{2,1,0:T(8,128)(2,1)}), bf16[32,64,768]{2,1,0:T(8,128)(2,1)S(1)}, u32[]{:S(2)}, u32[]{:S(2)}) %all-to-all-start.1) | async-done | bytes 3145760 | tf_op jit(solution)/shard_map/all_to_all | solution.py:9
  58.8 0.0 copy-start
  58.8 1.7 copy-done
  60.5 9.2 %all-to-all-start = ((bf16[32,64,768]{2,1,0:T(8,128)(2,1)}), bf16[32,64,768]{2,1,0:T(8,128)(2,1)S(1)}, u32[]{:S(2)}, u32[]{:S(2)}) async-start(bf16[32,64,768]{2,1,0:T(8,128)(2,1)} %add_convert_fusion.1), calls=%async_computation | async-start | bytes 6291456 | tf_op jit(solution)/shard_map/all_to_all | solution.py:9
  69.6 0.0 copy-done.1
  69.6 0.0 copy-done.2
  69.7 109.4 %all-gather = bf16[32,64,32]{1,2,0:T(8,128)(2,1)S(1)} all-gather(bf16[1,64,32]{1,2,0:T(8,128)(2,1)S(1)} %fusion.2), channel_id=1, replica_groups=mesh['bank'=4,'zero'=32] {'zero'}, dimensions={0}, use_global_device_ids=true | all-gather | bytes 135168 | tf_op jit(solution)/shard_map/all_gather | solution.py:22
  179.1 0.1 copy.13
  179.2 0.3 reshape.148
  179.5 21.2 %all_gather.7 = bf16[2048,128]{0,1:T(8,128)(2,1)} all-gather(bf16[2048,32]{0,1:T(8,128)(2,1)S(1)} %reshape.148), channel_id=1, replica_groups=mesh['bank'=4,'zero'=32] {'bank'}, dimensions={1}, use_global_device_ids=true | all-gather | bytes 655360 | tf_op jit(solution)/shard_map/all_gather | solution.py:23
  200.7 2.0 copy.14
  202.8 2.6 %multiply_reduce_fusion = f32[768]{0:T(1024)S(1)} fusion(bf16[32,64,768]{2,1,0:T(8,128)(2,1)} %copy-done), kind=kLoop, calls=%fused_computation.4 | loop fusion | flops 4717824 | bytes 3148800 | tf_op jit(solution)/shard_map/reduce_sum | solution.py:14
  205.4 0.6 sqrt.39
  206.0 2.7 %convert_element_type.89 = f32[32,64,768]{2,1,0:T(8,128)S(1)} convert(bf16[32,64,768]{2,1,0:T(8,128)(2,1)} %copy-done) | non-fusion elementwise | flops 1572864 | bytes 9437184 | tf_op jit(solution)/shard_map/convert_element_type | solution.py:13
  208.6 2.3 %fusion = bf16[1,2048,768]{2,1,0:T(8,128)(2,1)} fusion(f32[768]{0:T(1024)S(1)} %sqrt.37, f32[1,2048,768]{2,1,0:T(8,128)S(1)} %bitcast.14), kind=kLoop, calls=%fused_computation.1 | loop fusion | flops 3145728 | bytes 9440256 | tf_op jit(solution)/shard_map/convert_element_type | solution.py:15
  210.9 0.0 all-to-all-done
  210.9 0.7 multiply_reduce_fusion.1
  211.7 0.6 sqrt.38
  212.2 0.8 convert_element_type.88
  213.0 2.3 %fusion.1 = bf16[1,2048,768]{2,1,0:T(8,128)(2,1)} fusion(f32[768]{0:T(1024)S(1)} %sqrt.36, f32[1,2048,768]{2,1,0:T(8,128)S(1)} %bitcast.15), kind=kLoop, calls=%fused_computation.3 | loop fusion | flops 3145728 | bytes 9440256 | tf_op jit(solution)/shard_map/convert_element_type | solution.py:15
  (3 shorter events, 0.0 us)
Async XLA Ops:
  7.0 51.7 %all-to-all-start.1 = ((bf16[32,64,768]{2,1,0:T(8,128)(2,1)}), bf16[32,64,768]{2,1,0:T(8,128)(2,1)S(1)}, u32[]{:S(2)}, u32[]{:S(2)}) async-start(bf16[32,64,768]{2,1,0:T(8,128)(2,1)} %add_convert_fusion), calls=%async_computation.1 | async-start | bytes 6291456 | tf_op jit(solution)/shard_map/all_to_all | solution.py:9
  24.8 44.8 %copy-start.1 = (f32[64,32]{0,1:T(8,128)S(1)}, f32[64,32]{0,1:T(8,128)}, u32[]{:S(2)}) copy-start(f32[64,32]{0,1:T(8,128)} %param.10) | copy-start | bytes 24580
  24.8 44.8 %copy-start.2 = (f32[64]{0:T(128)S(1)}, f32[64]{0:T(128)}, u32[]{:S(2)}) copy-start(f32[64]{0:T(128)} %param.11) | copy-start | bytes 772
  58.8 1.7 copy-start
  60.5 150.5 %all-to-all-start = ((bf16[32,64,768]{2,1,0:T(8,128)(2,1)}), bf16[32,64,768]{2,1,0:T(8,128)(2,1)S(1)}, u32[]{:S(2)}, u32[]{:S(2)}) async-start(bf16[32,64,768]{2,1,0:T(8,128)(2,1)} %add_convert_fusion.1), calls=%async_computation | async-start | bytes 6291456 | tf_op jit(solution)/shard_map/all_to_all | solution.py:9
where the time goes:
time: 216 us; the launch traced here: 215 us
  blocking collectives  131 us (61%)
  waiting for transfers between devices  34 us (16%)
  other arithmetic  24.2 us (11%)
  starting transfers between devices  20.5 us (9%)
  local copies, waits for them, and re-layouts  5.28 us (2%)
    all_gather x1, blocking collectives, body(): serve_router = lax.all_gather(part_router, 'zero', axis=0, tiled=True)  109 us
    all_to_all x2, waiting for transfers between devices, regrouped(): lax.all_to_all(latest, 'zero', split_axis=0, concat_axis=1, tiled=True)  34 us
    all_gather x1, blocking collectives, body(): serve_router = lax.all_gather(serve_router, 'bank', axis=1, tiled=True)  21.2 us
    all_to_all x2, starting transfers between devices, regrouped(): lax.all_to_all(latest, 'zero', split_axis=0, concat_axis=1, tiled=True)  20.5 us
    convert_element_type x2, other arithmetic, regrouped(): latest = (train + other.astype(jnp.float32)).astype(jnp.bfloat16)  12.8 us
    convert_element_type x2, other arithmetic, normalised(): return ((wide / scale[:, None, :]).astype(jnp.bfloat16), scale)  4.52 us
  transfers between devices with their start and end apart: 2, of which 1 were waited for; matrix products, arithmetic and copies ran while one was open for 8% of the time, Pallas kernels for 0%

commit v1 on v0

--- a/solution.py
+++ b/solution.py
@@ -1,7 +1,16 @@
+import functools
 import jax
 import jax.numpy as jnp
 from jax import lax
 from jax.sharding import PartitionSpec as P
+from jax.lax import all_gather
+
+
+def _apply_flows(sheet, shard_axis):
+    return jnp.concatenate(all_gather(sheet, shard_axis), 1)
+
+
+_place_gates = functools.partial(_apply_flows, shard_axis="bank")
 
 
 def regrouped(train, other):
@@ -20,7 +29,7 @@
     up = regrouped(train_up, other_up)
     part_router = (router_weight * router_gain[:, None]).astype(jnp.bfloat16)
     serve_router = lax.all_gather(part_router, "zero", axis=0, tiled=True)
-    serve_router = lax.all_gather(serve_router, "bank", axis=1, tiled=True)
+    serve_router = _place_gates(serve_router)
     ready_gate, scale_gate = normalised(gate)
     ready_up, scale_up = normalised(up)
     return (ready_gate, ready_up, scale_gate, scale_up, serve_router)

time: 216 us -> 220 us (1.019)
  local copies, waits for them, and re-layouts: 5.28 us -> 9.61 us
    all_gather x0 -> x1, local copies, waits for them, and re-layouts: none -> 2.22 us  [_apply_flows(): return jnp.concatenate(all_gather(sheet, shard_axis), 1)]
  transfers between devices with their start and end apart: 2 -> 2, of which waited for: 1 -> 1; matrix products, arithmetic and copies ran while one was open for 8% -> 10% of each run, Pallas kernels for 0% -> 0%
where the time goes in v1:
time: 220 us
  blocking collectives  131 us (60%)
  waiting for transfers between devices  34 us (15%)
  other arithmetic  24.2 us (11%)
  starting transfers between devices  20.5 us (9%)
  local copies, waits for them, and re-layouts  9.61 us (4%)
    all_gather x1, blocking collectives, body(): serve_router = lax.all_gather(part_router, 'zero', axis=0, tiled=True)  109 us
    all_to_all x2, waiting for transfers between devices, regrouped(): lax.all_to_all(latest, 'zero', split_axis=0, concat_axis=1, tiled=True)  34 us
    all_gather x1, blocking collectives, _apply_flows(): return jnp.concatenate(all_gather(sheet, shard_axis), 1)  21.2 us
    all_to_all x2, starting transfers between devices, regrouped(): lax.all_to_all(latest, 'zero', split_axis=0, concat_axis=1, tiled=True)  20.5 us
    convert_element_type x2, other arithmetic, regrouped(): latest = (train + other.astype(jnp.float32)).astype(jnp.bfloat16)  12.8 us
    convert_element_type x2, other arithmetic, normalised(): return ((wide / scale[:, None, :]).astype(jnp.bfloat16), scale)  4.52 us
  transfers between devices with their start and end apart: 2, of which 1 were waited for; matrix products, arithmetic and copies ran while one was open for 10% of the time, Pallas kernels for 0%

profile of v1, /device:TPU:1, one launch (start us, length us, event | category | flops | bytes accessed | tf_op | source)
XLA Modules:
  0.0 219.6 jit_solution(15445600055573571469)
XLA Ops:
  0.6 6.4 %add_convert_fusion = bf16[32,64,768]{2,1,0:T(8,128)(2,1)} fusion(f32[32,64,768]{2,1,0:T(8,128)} %param.8, bf16[32,64,768]{2,1,0:T(8,128)(2,1)} %param.9), kind=kLoop, calls=%fused_computation.5 | loop fusion | flops 4718592 | bytes 12582912 | tf_op jit(solution)/shard_map/convert_element_type | solution.py:17
  7.0 11.3 %all-to-all-start.1 = ((bf16[32,64,768]{2,1,0:T(8,128)(2,1)}), bf16[32,64,768]{2,1,0:T(8,128)(2,1)S(1)}, u32[]{:S(2)}, u32[]{:S(2)}) async-start(bf16[32,64,768]{2,1,0:T(8,128)(2,1)} %add_convert_fusion), calls=%async_computation.1 | async-start | bytes 6291456 | tf_op jit(solution)/shard_map/all_to_all | solution.py:18
  18.4 6.4 %add_convert_fusion.1 = bf16[32,64,768]{2,1,0:T(8,128)(2,1)} fusion(f32[32,64,768]{2,1,0:T(8,128)} %param.6, bf16[32,64,768]{2,1,0:T(8,128)(2,1)} %param.7), kind=kLoop, calls=%fused_computation.7 | loop fusion | flops 4718592 | bytes 12582912 | tf_op jit(solution)/shard_map/convert_element_type | solution.py:17
  24.8 0.0 copy-start.1
  24.8 0.0 copy-start.2
  24.8 34.0 %all-to-all-done.1 = bf16[32,64,768]{2,1,0:T(8,128)(2,1)S(1)} async-done(((bf16[32,64,768]{2,1,0:T(8,128)(2,1)}), bf16[32,64,768]{2,1,0:T(8,128)(2,1)S(1)}, u32[]{:S(2)}, u32[]{:S(2)}) %all-to-all-start.1) | async-done | bytes 3145760 | tf_op jit(solution)/shard_map/all_to_all | solution.py:18
  58.8 0.0 copy-start
  58.8 1.7 copy-done
  60.5 9.2 %all-to-all-start = ((bf16[32,64,768]{2,1,0:T(8,128)(2,1)}), bf16[32,64,768]{2,1,0:T(8,128)(2,1)S(1)}, u32[]{:S(2)}, u32[]{:S(2)}) async-start(bf16[32,64,768]{2,1,0:T(8,128)(2,1)} %add_convert_fusion.1), calls=%async_computation | async-start | bytes 6291456 | tf_op jit(solution)/shard_map/all_to_all | solution.py:18
  69.6 0.0 copy-done.1
  69.6 0.0 copy-done.2
  69.7 109.4 %all-gather.1 = bf16[32,64,32]{1,2,0:T(8,128)(2,1)S(1)} all-gather(bf16[1,64,32]{1,2,0:T(8,128)(2,1)S(1)} %fusion.2), channel_id=1, replica_groups=mesh['bank'=4,'zero'=32] {'zero'}, dimensions={0}, use_global_device_ids=true | all-gather | bytes 135168 | tf_op jit(solution)/shard_map/all_gather | solution.py:31
  179.1 0.1 copy.14
  179.2 0.3 reshape.157
  179.5 21.2 %all-gather = bf16[8192,32]{0,1:T(8,128)(2,1)} all-gather(bf16[2048,32]{0,1:T(8,128)(2,1)S(1)} %reshape.157), channel_id=2, replica_groups=mesh['bank'=4,'zero'=32] {'bank'}, dimensions={0}, use_global_device_ids=true | all-gather | bytes 655360 | tf_op jit(solution)/shard_map/all_gather | solution.py:10
  200.7 2.2 %reshape.155 = bf16[4,2048,32]{1,0,2:T(4,128)(2,1)} reshape(bf16[8192,32]{0,1:T(8,128)(2,1)} %all-gather) | data formatting | bytes 1048576 | tf_op jit(solution)/shard_map/all_gather | solution.py:10
  202.9 2.1 copy.15
  205.0 2.0 copy.16
  207.1 2.6 %multiply_reduce_fusion = f32[768]{0:T(1024)S(1)} fusion(bf16[32,64,768]{2,1,0:T(8,128)(2,1)} %copy-done), kind=kLoop, calls=%fused_computation.4 | loop fusion | flops 4717824 | bytes 3148800 | tf_op jit(solution)/shard_map/reduce_sum | solution.py:23
  209.7 0.6 sqrt.39
  210.3 2.7 %convert_element_type.89 = f32[32,64,768]{2,1,0:T(8,128)S(1)} convert(bf16[32,64,768]{2,1,0:T(8,128)(2,1)} %copy-done) | non-fusion elementwise | flops 1572864 | bytes 9437184 | tf_op jit(solution)/shard_map/convert_element_type | solution.py:22
  213.0 2.3 %fusion = bf16[1,2048,768]{2,1,0:T(8,128)(2,1)} fusion(f32[768]{0:T(1024)S(1)} %sqrt.37, f32[1,2048,768]{2,1,0:T(8,128)S(1)} %bitcast.18), kind=kLoop, calls=%fused_computation.1 | loop fusion | flops 3145728 | bytes 9440256 | tf_op jit(solution)/shard_map/convert_element_type | solution.py:24
  215.2 0.0 all-to-all-done
  215.2 0.7 multiply_reduce_fusion.1
  216.0 0.6 sqrt.38
  216.6 0.8 convert_element_type.88
  217.4 2.3 %fusion.1 = bf16[1,2048,768]{2,1,0:T(8,128)(2,1)} fusion(f32[768]{0:T(1024)S(1)} %sqrt.36, f32[1,2048,768]{2,1,0:T(8,128)S(1)} %bitcast.19), kind=kLoop, calls=%fused_computation.3 | loop fusion | flops 3145728 | bytes 9440256 | tf_op jit(solution)/shard_map/convert_element_type | solution.py:24
  (3 shorter events, 0.0 us)
Async XLA Ops:
  7.0 51.7 %all-to-all-start.1 = ((bf16[32,64,768]{2,1,0:T(8,128)(2,1)}), bf16[32,64,768]{2,1,0:T(8,128)(2,1)S(1)}, u32[]{:S(2)}, u32[]{:S(2)}) async-start(bf16[32,64,768]{2,1,0:T(8,128)(2,1)} %add_convert_fusion), calls=%async_computation.1 | async-start | bytes 6291456 | tf_op jit(solution)/shard_map/all_to_all | solution.py:18
  24.8 44.8 %copy-start.1 = (f32[64,32]{0,1:T(8,128)S(1)}, f32[64,32]{0,1:T(8,128)}, u32[]{:S(2)}) copy-start(f32[64,32]{0,1:T(8,128)} %param.10) | copy-start | bytes 24580
  24.8 44.8 %copy-start.2 = (f32[64]{0:T(128)S(1)}, f32[64]{0:T(128)}, u32[]{:S(2)}) copy-start(f32[64]{0:T(128)} %param.11) | copy-start | bytes 772
  58.8 1.7 copy-start
  60.5 154.8 %all-to-all-start = ((bf16[32,64,768]{2,1,0:T(8,128)(2,1)}), bf16[32,64,768]{2,1,0:T(8,128)(2,1)S(1)}, u32[]{:S(2)}, u32[]{:S(2)}) async-start(bf16[32,64,768]{2,1,0:T(8,128)(2,1)} %add_convert_fusion.1), calls=%async_computation | async-start | bytes 6291456 | tf_op jit(solution)/shard_map/all_to_all | solution.py:18

commit v2 on v0

--- a/solution.py
+++ b/solution.py
@@ -1,7 +1,21 @@
+import functools
 import jax
 import jax.numpy as jnp
 from jax import lax
 from jax.sharding import PartitionSpec as P
+
+
+def change_vector(vec, device_axis):
+    found = []
+    for _ in range(lax.axis_size(device_axis)):
+        found.append(vec)
+    block_out = jnp.stack(found)
+    upper = lax.all_to_all(block_out, split_axis=0, axis_name=device_axis, concat_axis=0)
+    big = jnp.concatenate(upper, axis=0)
+    return big
+
+
+list_results_on = functools.partial(change_vector, device_axis="zero")
 
 
 def regrouped(train, other):
@@ -19,7 +33,7 @@
     gate = regrouped(train_gate, other_gate)
     up = regrouped(train_up, other_up)
     part_router = (router_weight * router_gain[:, None]).astype(jnp.bfloat16)
-    serve_router = lax.all_gather(part_router, "zero", axis=0, tiled=True)
+    serve_router = list_results_on(part_router)
     serve_router = lax.all_gather(serve_router, "bank", axis=1, tiled=True)
     ready_gate, scale_gate = normalised(gate)
     ready_up, scale_up = normalised(up)

time: 216 us -> 142 us (0.66)
  the two profiles are of different devices: /device:TPU:1 before, /device:TPU:19 now
where the time goes in v2:
time: 142 us; the launch traced here: 141 us
  blocking collectives  44.2 us (31%)
  waiting for transfers between devices  38.2 us (27%)
  starting transfers between devices  25.5 us (18%)
  other arithmetic  24.9 us (18%)
  local copies, waits for them, and re-layouts  8.03 us (6%)
    all_gather x1, blocking collectives, body(): serve_router = lax.all_gather(serve_router, 'bank', axis=1, tiled=True)  44.2 us
    all_to_all x2, waiting for transfers between devices, regrouped(): lax.all_to_all(latest, 'zero', split_axis=0, concat_axis=1, tiled=True)  38.2 us
    all_to_all x2, starting transfers between devices, regrouped(): lax.all_to_all(latest, 'zero', split_axis=0, concat_axis=1, tiled=True)  15.2 us
    convert_element_type x2, other arithmetic, regrouped(): latest = (train + other.astype(jnp.float32)).astype(jnp.bfloat16)  12.8 us
    all_to_all x1, starting transfers between devices, change_vector(): lax.all_to_all(block_out, split_axis=0, axis_name=device_axis, concat_axi...  10.3 us
    unnamed x6, local copies, waits for them, and re-layouts  4.81 us
    convert_element_type x2, other arithmetic, normalised(): return ((wide / scale[:, None, :]).astype(jnp.bfloat16), scale)  4.52 us
    convert_element_type x2, other arithmetic, normalised(): wide = pieces.astype(jnp.float32)  3.44 us
  transfers between devices with their start and end apart: 3, of which 1 were waited for; matrix products, arithmetic and copies ran while one was open for 18% of the time, Pallas kernels for 0%

profile of v2, /device:TPU:19, one launch (start us, length us, event | category | flops | bytes accessed | tf_op | source)
XLA Modules:
  0.0 141.4 jit_solution(12718003715768044233)
XLA Ops:
  0.6 0.7 multiply_convert_fusion
  1.4 0.8 reshape.153
  2.2 10.3 %all-to-all-start.2 = ((bf16[32,2,1024]{2,1,0:T(2,128)(2,1)}), bf16[32,2,1024]{2,1,0:T(2,128)(2,1)S(1)}, u32[]{:S(2)}, u32[]{:S(2)}) async-start(bf16[32,2,1024]{2,1,0:T(2,128)(2,1)} %reshape.153), calls=%async_computation.2 | async-start | bytes 262144 | tf_op jit(solution)/shard_map/all_to_all | solution.py:13
  12.6 6.4 %add_convert_fusion = bf16[32,64,768]{2,1,0:T(8,128)(2,1)} fusion(f32[32,64,768]{2,1,0:T(8,128)} %param.8, bf16[32,64,768]{2,1,0:T(8,128)(2,1)} %param.9), kind=kLoop, calls=%fused_computation.5 | loop fusion | flops 4718592 | bytes 12582912 | tf_op jit(solution)/shard_map/convert_element_type | solution.py:22
  19.0 0.0 all-to-all-done.2
  19.0 9.2 %all-to-all-start.1 = ((bf16[32,64,768]{2,1,0:T(8,128)(2,1)}), bf16[32,64,768]{2,1,0:T(8,128)(2,1)S(1)}, u32[]{:S(2)}, u32[]{:S(2)}) async-start(bf16[32,64,768]{2,1,0:T(8,128)(2,1)} %add_convert_fusion), calls=%async_computation.1 | async-start | bytes 6291456 | tf_op jit(solution)/shard_map/all_to_all | solution.py:23
  28.2 6.4 %add_convert_fusion.1 = bf16[32,64,768]{2,1,0:T(8,128)(2,1)} fusion(f32[32,64,768]{2,1,0:T(8,128)} %param.6, bf16[32,64,768]{2,1,0:T(8,128)(2,1)} %param.7), kind=kLoop, calls=%fused_computation.7 | loop fusion | flops 4718592 | bytes 12582912 | tf_op jit(solution)/shard_map/convert_element_type | solution.py:22
  34.6 38.2 %all-to-all-done.1 = bf16[32,64,768]{2,1,0:T(8,128)(2,1)S(1)} async-done(((bf16[32,64,768]{2,1,0:T(8,128)(2,1)}), bf16[32,64,768]{2,1,0:T(8,128)(2,1)S(1)}, u32[]{:S(2)}, u32[]{:S(2)}) %all-to-all-start.1) | async-done | bytes 3145760 | tf_op jit(solution)/shard_map/all_to_all | solution.py:23
  72.8 0.0 copy-start
  72.8 1.7 %copy-done = bf16[32,64,768]{2,1,0:T(8,128)(2,1)} copy-done((bf16[32,64,768]{2,1,0:T(8,128)(2,1)}, bf16[32,64,768]{2,1,0:T(8,128)(2,1)S(1)}, u32[]{:S(2)}) %copy-start) | copy-done | bytes 3145752
  74.5 5.9 %all-to-all-start = ((bf16[32,64,768]{2,1,0:T(8,128)(2,1)}), bf16[32,64,768]{2,1,0:T(8,128)(2,1)S(1)}, u32[]{:S(2)}, u32[]{:S(2)}) async-start(bf16[32,64,768]{2,1,0:T(8,128)(2,1)} %add_convert_fusion.1), calls=%async_computation | async-start | bytes 6291456 | tf_op jit(solution)/shard_map/all_to_all | solution.py:23
  80.4 0.2 reshape.154
  80.6 0.8 copy.13
  81.4 1.2 reshape.150
  82.7 44.2 %all_gather.3 = bf16[2048,128]{0,1:T(8,128)(2,1)} all-gather(bf16[2048,32]{0,1:T(8,128)(2,1)S(1)} %reshape.150), channel_id=1, replica_groups=mesh['bank'=4,'zero'=32] {'bank'}, dimensions={1}, use_global_device_ids=true | all-gather | bytes 655360 | tf_op jit(solution)/shard_map/all_gather | solution.py:37
  126.9 2.0 %copy.14 = bf16[2048,128]{1,0:T(8,128)(2,1)} copy(bf16[2048,128]{0,1:T(8,128)(2,1)} %all_gather.3) | data formatting | bytes 1048576
  128.9 2.6 %multiply_reduce_fusion = f32[768]{0:T(1024)S(1)} fusion(bf16[32,64,768]{2,1,0:T(8,128)(2,1)} %copy-done), kind=kLoop, calls=%fused_computation.4 | loop fusion | flops 4717824 | bytes 3148800 | tf_op jit(solution)/shard_map/reduce_sum | solution.py:28
  131.5 0.6 sqrt.39
  132.1 2.7 %convert_element_type.89 = f32[32,64,768]{2,1,0:T(8,128)S(1)} convert(bf16[32,64,768]{2,1,0:T(8,128)(2,1)} %copy-done) | non-fusion elementwise | flops 1572864 | bytes 9437184 | tf_op jit(solution)/shard_map/convert_element_type | solution.py:27
  134.8 2.3 %fusion = bf16[1,2048,768]{2,1,0:T(8,128)(2,1)} fusion(f32[768]{0:T(1024)S(1)} %sqrt.37, f32[1,2048,768]{2,1,0:T(8,128)S(1)} %bitcast.15), kind=kLoop, calls=%fused_computation.1 | loop fusion | flops 3145728 | bytes 9440256 | tf_op jit(solution)/shard_map/convert_element_type | solution.py:29
  137.1 0.0 all-to-all-done
  137.1 0.7 multiply_reduce_fusion.1
  137.8 0.6 sqrt.38
  138.4 0.8 convert_element_type.88
  139.2 2.3 %fusion.1 = bf16[1,2048,768]{2,1,0:T(8,128)(2,1)} fusion(f32[768]{0:T(1024)S(1)} %sqrt.36, f32[1,2048,768]{2,1,0:T(8,128)S(1)} %bitcast.16), kind=kLoop, calls=%fused_computation.3 | loop fusion | flops 3145728 | bytes 9440256 | tf_op jit(solution)/shard_map/convert_element_type | solution.py:29
  (3 shorter events, 0.1 us)
Async XLA Ops:
  2.2 16.7 %all-to-all-start.2 = ((bf16[32,2,1024]{2,1,0:T(2,128)(2,1)}), bf16[32,2,1024]{2,1,0:T(2,128)(2,1)S(1)}, u32[]{:S(2)}, u32[]{:S(2)}) async-start(bf16[32,2,1024]{2,1,0:T(2,128)(2,1)} %reshape.153), calls=%async_computation.2 | async-start | bytes 262144 | tf_op jit(solution)/shard_map/all_to_all | solution.py:13
  19.0 53.8 %all-to-all-start.1 = ((bf16[32,64,768]{2,1,0:T(8,128)(2,1)}), bf16[32,64,768]{2,1,0:T(8,128)(2,1)S(1)}, u32[]{:S(2)}, u32[]{:S(2)}) async-start(bf16[32,64,768]{2,1,0:T(8,128)(2,1)} %add_convert_fusion), calls=%async_computation.1 | async-start | bytes 6291456 | tf_op jit(solution)/shard_map/all_to_all | solution.py:23
  72.8 1.7 %copy-start = (bf16[32,64,768]{2,1,0:T(8,128)(2,1)}, bf16[32,64,768]{2,1,0:T(8,128)(2,1)S(1)}, u32[]{:S(2)}) copy-start(bf16[32,64,768]{2,1,0:T(8,128)(2,1)S(1)} %all-to-all-done.1) | copy-start | bytes 9437188
  74.5 62.6 %all-to-all-start = ((bf16[32,64,768]{2,1,0:T(8,128)(2,1)}), bf16[32,64,768]{2,1,0:T(8,128)(2,1)S(1)}, u32[]{:S(2)}, u32[]{:S(2)}) async-start(bf16[32,64,768]{2,1,0:T(8,128)(2,1)} %add_convert_fusion.1), calls=%async_computation | async-start | bytes 6291456 | tf_op jit(solution)/shard_map/all_to_all | solution.py:23
